TPU v7x, 32 devices: a whole 2x2x4 slice. The times are simulated.
32 devices in a mesh: rep: 16 (over z, x, core), tp: 2 (over y).
Axes of the slice: x: 2, y: 2, z: 4, core: 2. Of those that a mesh axis runs over, the one named last changes fastest.
Arguments:
- tokens: bfloat16 [16, 256, 3072], P('rep', 'tp'), may hold values from -100 to 100
- norm_gain: float32 [16, 3072], P('rep'), may hold values from 0.5 to 1.5
- w_query: bfloat16 [16, 3072, 2048], P('rep', None, 'tp'), may hold values from -1 to 1
- key_weight: bfloat16 [16, 3072, 1024], P('rep', None, 'tp'), may hold values from -1 to 1
- value_weight: bfloat16 [16, 3072, 1024], P('rep', None, 'tp'), may hold values from -0.109375 to 0.109375
- attention_gradient: bfloat16 [16, 256, 2048], P('rep', None, 'tp'), may hold values from -6 to 6
- global_fragment: float32 [128, 3072], P('tp'), may hold values from -6 to 6
- momentum: float32 [128, 3072], P('tp'), may hold values from -3 to 3
- local_fragment: bfloat16 [16, 128, 3072], P('rep', 'tp'), may hold values from -6 to 6
Outputs:
- grad_query_w: bfloat16 [16, 3072, 2048], P('rep', None, 'tp')
- grad_key_w: bfloat16 [16, 3072, 1024], P('rep', None, 'tp')
- grad_value_w: bfloat16 [16, 3072, 1024], P('rep', None, 'tp')
- grad_gain: float32 [16, 3072], P('rep')
- grad_tokens: bfloat16 [16, 256, 3072], P('rep', 'tp')
- new_global: float32 [128, 3072], P('tp')
- new_momentum: float32 [128, 3072], P('tp')
All inputs are finite; a program needn't handle non-finite values.
Results may differ from a plain program's by a relative error of at most 0.019.
The roundings to bfloat16 on the way count: a program that leaves them out, or rounds other values in their place, can miss the bound.
Values may be sent and summed in bfloat16 or wider, within the bound.
A program may use at most 128 MiB of HBM per device.

v0:
```python
import jax
import jax.numpy as jnp
from jax import lax
from jax.sharding import PartitionSpec as P

HEAD_SIZE = 128
epsilon = 1e-05
rope_base = 500000.0
outer_rate = 0.7
outer_momentum = 0.9


def rope_tables(sequence_length, width):
    middle = width // 2
    frequency = rope_base ** (-2.0 * jnp.arange(middle, dtype=jnp.float32) / width)
    angles = jnp.arange(sequence_length, dtype=jnp.float32)[:, None] * frequency[None, :]
    angles = jnp.concatenate([angles, angles], axis=1)
    return (jnp.cos(angles)[:, None, :], jnp.sin(angles)[:, None, :])


def rotate(vectors, cosine_table, sine_table):
    middle = vectors.shape[-1] // 2
    turned = jnp.concatenate([-vectors[..., middle:], vectors[..., :middle]], axis=-1)
    return vectors * cosine_table + turned * sine_table


def reverse_rotation(gradient, cosine_table, sine_table):
    middle = gradient.shape[-1] // 2
    shifted = gradient * sine_table
    turned = jnp.concatenate([shifted[..., middle:], -shifted[..., :middle]], axis=-1)
    return gradient * cosine_table + turned


def attention_reverse(query_rows, rotated_keys, values_bfloat, grad_out, block_of_rows):
    sequence_length = query_rows.shape[0]
    score_scale = query_rows.shape[-1] ** (-0.5)

    def one_block(running, block_index):
        acc_key, acc_value = running
        offset = block_index * block_of_rows
        query_block = lax.dynamic_slice_in_dim(query_rows, offset, block_of_rows, 0)
        grad_block = lax.dynamic_slice_in_dim(grad_out, offset, block_of_rows, 0)
        scores = (
            jnp.einsum(
                "qgrd,kgd->grqk", query_block, rotated_keys, preferred_element_type=jnp.float32
            )
            * score_scale
        )
        row_pos = offset + jnp.arange(block_of_rows)
        col_pos = jnp.arange(sequence_length)
        allowed = col_pos[None, :] <= row_pos[:, None]
        scores = jnp.where(allowed, scores, -jnp.inf)
        highest = jnp.max(scores, axis=-1, keepdims=True)
        powers = jnp.exp(scores - highest)
        probability = powers / jnp.sum(powers, axis=-1, keepdims=True)
        prob_low = probability.astype(jnp.bfloat16)
        acc_value = acc_value + jnp.einsum(
            "grqk,qgrd->kgd", prob_low, grad_block, preferred_element_type=jnp.float32
        )
        grad_prob = jnp.einsum(
            "qgrd,kgd->grqk", grad_block, values_bfloat, preferred_element_type=jnp.float32
        )
        grad_score = (
            probability
            * (grad_prob - jnp.sum(grad_prob * probability, axis=-1, keepdims=True))
            * score_scale
        )
        score_low = grad_score.astype(jnp.bfloat16)
        grad_query = jnp.einsum(
            "grqk,kgd->qgrd", score_low, rotated_keys, preferred_element_type=jnp.float32
        )
        acc_key = acc_key + jnp.einsum(
            "grqk,qgrd->kgd", score_low, query_block, preferred_element_type=jnp.float32
        )
        return ((acc_key, acc_value), grad_query)

    initial = jnp.zeros(rotated_keys.shape, jnp.float32)
    (acc_key, acc_value), grad_blocks = lax.scan(
        one_block, (initial, initial), jnp.arange(sequence_length // block_of_rows)
    )
    return (grad_blocks.reshape(query_rows.shape), acc_key, acc_value)


def body(
    tokens,
    norm_gain,
    w_query,
    key_weight,
    value_weight,
    attention_gradient,
    global_fragment,
    momentum,
    local_fragment,
):
    local_rows = tokens[0]
    norm_gains = norm_gain[0]
    weight_q = w_query[0]
    weight_k = key_weight[0]
    weight_v = value_weight[0]
    widened_rows = local_rows.astype(jnp.float32)
    inverse_norm = lax.rsqrt(
        jnp.mean(widened_rows * widened_rows, axis=-1, keepdims=True) + epsilon
    )
    normalized_input = widened_rows * inverse_norm
    normalized_local = (normalized_input * norm_gains[None, :]).astype(jnp.bfloat16)
    normalized = lax.all_gather(normalized_local, "tp", axis=0, tiled=True)
    sequence_length = normalized.shape[0]
    heads_q = weight_q.shape[1] // HEAD_SIZE
    heads_kv = weight_k.shape[1] // HEAD_SIZE
    cosine_table, sine_table = rope_tables(sequence_length, HEAD_SIZE)
    query_rows = jnp.dot(normalized, weight_q, preferred_element_type=jnp.float32).reshape(
        sequence_length, heads_q, HEAD_SIZE
    )
    query_rows = rotate(query_rows, cosine_table, sine_table).astype(jnp.bfloat16)
    rotated_keys = jnp.dot(normalized, weight_k, preferred_element_type=jnp.float32).reshape(
        sequence_length, heads_kv, HEAD_SIZE
    )
    rotated_keys = rotate(rotated_keys, cosine_table, sine_table).astype(jnp.bfloat16)
    values_bfloat = (
        jnp.dot(normalized, weight_v, preferred_element_type=jnp.float32)
        .astype(jnp.bfloat16)
        .reshape(sequence_length, heads_kv, HEAD_SIZE)
    )
    replica_group = heads_q // heads_kv
    block_of_rows = min(512, sequence_length)
    query_input_gradient, key_input_gradient, value_input_gradient = attention_reverse(
        query_rows.reshape(sequence_length, heads_kv, replica_group, HEAD_SIZE),
        rotated_keys,
        values_bfloat,
        attention_gradient[0].reshape(sequence_length, heads_kv, replica_group, HEAD_SIZE),
        block_of_rows,
    )
    dquery = (
        reverse_rotation(
            query_input_gradient.reshape(sequence_length, heads_q, HEAD_SIZE),
            cosine_table,
            sine_table,
        )
        .astype(jnp.bfloat16)
        .reshape(sequence_length, heads_q * HEAD_SIZE)
    )
    key_gradient = (
        reverse_rotation(key_input_gradient, cosine_table, sine_table)
        .astype(jnp.bfloat16)
        .reshape(sequence_length, heads_kv * HEAD_SIZE)
    )
    value_gradient = value_input_gradient.astype(jnp.bfloat16).reshape(
        sequence_length, heads_kv * HEAD_SIZE
    )
    contract = (((0,), (0,)), ((), ()))
    grad_wq = lax.dot_general(
        normalized, dquery, contract, preferred_element_type=jnp.float32
    ).astype(jnp.bfloat16)
    grad_wk = lax.dot_general(
        normalized, key_gradient, contract, preferred_element_type=jnp.float32
    ).astype(jnp.bfloat16)
    grad_wv = lax.dot_general(
        normalized, value_gradient, contract, preferred_element_type=jnp.float32
    ).astype(jnp.bfloat16)
    back = (((1,), (1,)), ((), ()))
    partial_value = lax.dot_general(dquery, weight_q, back, preferred_element_type=jnp.float32)
    partial_value = partial_value + lax.dot_general(
        key_gradient, weight_k, back, preferred_element_type=jnp.float32
    )
    summed_rows = lax.psum_scatter(
        (
            partial_value
            + lax.dot_general(value_gradient, weight_v, back, preferred_element_type=jnp.float32)
        ).astype(jnp.bfloat16),
        "tp",
        scatter_dimension=0,
        tiled=True,
    ).astype(jnp.float32)
    gains_gradient = lax.psum(jnp.sum(summed_rows * normalized_input, axis=0), "tp")
    scaled_rows = summed_rows * norm_gains[None, :]
    gradient_rows = (
        inverse_norm
        * (
            scaled_rows
            - normalized_input * jnp.mean(scaled_rows * normalized_input, axis=-1, keepdims=True)
        )
    ).astype(jnp.bfloat16)
    delta = global_fragment - local_fragment[0].astype(jnp.float32)
    replicas = lax.axis_size("rep")
    mean_delta = lax.psum(delta, "rep") / replicas
    new_momentum = outer_momentum * momentum + mean_delta
    new_global = global_fragment - outer_rate * (mean_delta + outer_momentum * new_momentum)
    return (
        grad_wq[None],
        grad_wk[None],
        grad_wv[None],
        gains_gradient[None],
        gradient_rows[None],
        new_global,
        new_momentum,
    )


def solution(mesh):
    placed = (
        P("rep", "tp", None),
        P("rep", None),
        P("rep", None, "tp"),
        P("rep", None, "tp"),
        P("rep", None, "tp"),
        P("rep", None, "tp"),
        P("tp", None),
        P("tp", None),
        P("rep", "tp", None),
    )
    return jax.shard_map(
        body,
        mesh=mesh,
        in_specs=placed,
        out_specs=(
            P("rep", None, "tp"),
            P("rep", None, "tp"),
            P("rep", None, "tp"),
            P("rep", None),
            P("rep", "tp", None),
            P("tp", None),
            P("tp", None),
        ),
        check_vma=False,
    )
```

profile of v0, /device:TPU:0, one launch (start us, length us, event | category | flops | bytes accessed | tf_op | source)
XLA Modules:
  0.0 146.9 jit_solution(9005998716346742518)
XLA Ops:
  8.1 1.6 %fusion.25 = f32[128]{0:T(128)S(1)} fusion(bf16[1,128,3072]{2,1,0:T(8,128)(2,1)} %param.9), kind=kLoop, calls=%fused_computation.37 | loop fusion | flops 1179520 | bytes 786944 | tf_op jit(solution)/shard_map/reduce_sum | solution.py:102
  9.6 2.3 %fusion.22 = bf16[128,3072]{1,0:T(8,128)(2,1)} fusion(bf16[1,128,3072]{2,1,0:T(8,128)(2,1)} %param.9, f32[3072]{0:T(1024)} %bitcast.153, f32[128]{0:T(128)S(1)} %add_rsqrt_fusion), kind=kLoop, calls=%fused_computation.34 | loop fusion | flops 1572864 | bytes 1585664 | tf_op jit(solution)/shard_map/convert_element_type | solution.py:105
  12.0 2.1 %convert_subtract_fusion = f32[64,3072]{1,0:T(8,128)} fusion(f32[64,3072]{1,0:T(8,128)} %param.15, bf16[1,64,3072]{2,1,0:T(8,128)(2,1)S(1)} %copy-done.19), kind=kLoop, calls=%fused_computation.65 | loop fusion | flops 393216 | bytes 1966080 | tf_op jit(solution)/shard_map/sub | solution.py:183
  14.2 8.7 %copy.38 = bf16[1024,3072]{1,0:T(8,128)(2,1)} copy(bf16[1024,3072]{0,1:T(8,128)(2,1)} %bitcast.138) | data formatting | bytes 12582912 | tf_op jit(solution)/shard_map/dot_general | solution.py:111
  23.4 4.7 %copy.35 = bf16[512,3072]{1,0:T(8,128)(2,1)} copy(bf16[512,3072]{0,1:T(8,128)(2,1)} %bitcast.137) | data formatting | bytes 6291456 | tf_op jit(solution)/shard_map/dot_general | solution.py:115
  28.1 2.0 %copy.41 = bf16[1,256,1024]{1,2,0:T(8,128)(2,1)} copy(bf16[1,256,1024]{2,1,0:T(8,128)(2,1)} %param.14) | data formatting | bytes 1048576 | tf_op jit(solution)/shard_map/reshape;squeeze | solution.py:130
  30.2 11.8 %all-gather.2.cloned.1.call-done = bf16[256,3072]{1,0:T(8,128)(2,1)} async-done(((bf16[128,3072]{1,0:T(8,128)(2,1)}), bf16[256,3072]{1,0:T(8,128)(2,1)}) %all-gather.2.cloned.1.call-update) | async-done | bytes 1572880 | tf_op jit(solution)/shard_map/all_gather | solution.py:106
  42.0 5.3 %fusion.26 = f32[256,8,128]{0,2,1:T(8,128)S(1)} fusion(bf16[8,128,3072]{2,1,0:T(8,128)(2,1)} %bitcast.141, bf16[256,3072]{1,0:T(8,128)(2,1)} %all-gather.2.cloned.1.call-done), kind=kOutput, calls=%fused_computation.38 | convolution fusion | flops 1610612736 | bytes 8912896 | tf_op jit(solution)/shard_map/dot_general | solution.py:111
  47.3 1.1 slice_negate_fusion.1
  48.4 1.1 copy-done.1
  51.5 1.7 %fusion.30 = bf16[256,512]{1,0:T(8,128)(2,1)} fusion(bf16[256,3072]{1,0:T(8,128)(2,1)S(1)} %copy-done.1, bf16[1,3072,512]{2,1,0:T(8,128)(2,1)S(1)} %copy-done), kind=kOutput, calls=%fused_computation.44 | convolution fusion | flops 805437440 | bytes 4980736 | tf_op jit(solution)/shard_map/dot_general | solution.py:120
  53.2 1.7 %reshape.115 = bf16[256,4,128]{2,1,0:T(4,128)(2,1)} reshape(bf16[256,512]{1,0:T(8,128)(2,1)} %fusion.30) | data formatting | bytes 524288 | tf_op jit(solution)/shard_map/reshape | solution.py:122
  55.0 2.7 %fusion.35 = bf16[256,8,128]{0,2,1:T(8,128)(2,1)} fusion(f32[256,8,64]{0,2,1:T(8,128)} %get-tuple-element.40, f32[256,8,64]{0,2,1:T(8,128)} %get-tuple-element.39, f32[256,8,128]{0,2,1:T(8,128)} %copy-done.7, f32[256,128]{0,1:T(8,128)S(1)} %get-tuple-element.46, f32[256,128]{0,1:T(8,128)S(1)} %get-tuple-element.45), kind=kLoop, calls=%fused_computation.48 | loop fusion | flops 1310720 | bytes 2883584 | tf_op jit(solution)/shard_map/convert_element_type | solution.py:114
  58.5 1.7 %fusion.51 = f32[4,256,256,2]{2,1,3,0:T(8,128)} fusion(bf16[256,4,2,128]{0,3,2,1:T(8,128)(2,1)S(1)} %bitcast.146, bf16[256,4,128,1]{2,1,0,3:T(4,128)(2,1)S(1)} %bitcast.149), kind=kOutput, calls=%fused_computation.78 | convolution fusion | flops 134217728 | bytes 2883584 | tf_op jit(solution)/shard_map/while/body/eval_jaxpr/qgrd,kgd->grqk/dot_general | solution.py:60
  60.2 3.3 %fusion.65 = (f32[4,2,256]{2,1,0:T(2,128)S(1)}, f32[4,2,256,256]{2,3,1,0:T(8,128)}) fusion(pred[256,256]{0,1:T(8,128)(4,1)S(1)} %iota_compare_fusion, bf16[256,4,128,1]{0,2,3,1:T(8,128)(2,1)} %fusion.50, bf16[256,4,2,128]{0,3,2,1:T(8,128)(2,1)} %bitcast.150), kind=kOutput, calls=%fused_computation.98 | convolution fusion | flops 136315136 | bytes 2957312 | tf_op jit(solution)/shard_map/while/body/eval_jaxpr/sub | solution.py:54
  63.5 5.4 %broadcast_multiply_fusion = (f32[256,4,128]{0,2,1:T(8,128)}, f32[256,4,128]{0,2,1:T(8,128)}) fusion(f32[256,128]{0,1:T(8,128)S(1)} %get-tuple-element.46, bf16[256,4,2,128]{0,3,2,1:T(8,128)(2,1)} %bitcast.151, f32[4,256,256,2]{2,1,3,0:T(8,128)} %fusion.51, f32[4,2,256,256]{2,3,1,0:T(8,128)} %get-tuple-element.48, f32[4,2,256]{2,1,0:T(2,128)S(1)} %get-tuple-element.47), kind=kOutput, calls=%fused_computation.81 | convolution fusion | flops 138021120 | bytes 5906432 | tf_op jit(solution)/shard_map/while/body/eval_jaxpr/grqk,qgrd->kgd/dot_general | solution.py:72
  68.8 5.3 %fusion.44 = f32[4,128,2,256]{3,1,2,0:T(8,128)} fusion(bf16[256,4,128,1]{0,2,3,1:T(8,128)(2,1)} %fusion.50, f32[4,256,256,2]{2,1,3,0:T(8,128)} %fusion.51, f32[4,2,256,256]{2,3,1,0:T(8,128)} %get-tuple-element.48, f32[4,2,256]{2,1,0:T(2,128)S(1)} %get-tuple-element.47), kind=kOutput, calls=%fused_computation.62 | convolution fusion | flops 137890048 | bytes 5513216 | tf_op jit(solution)/shard_map/while/body/eval_jaxpr/grqk,kgd->qgrd/dot_general | solution.py:69
  74.2 2.3 %fusion.33 = bf16[4,256,128]{1,2,0:T(8,128)(2,1)S(1)} fusion(bf16[256,4,2,128]{0,3,2,1:T(8,128)(2,1)} %bitcast.145, f32[4,2,256,256]{2,3,1,0:T(8,128)} %get-tuple-element.48, f32[4,2,256]{2,1,0:T(2,128)S(1)} %get-tuple-element.47), kind=kOutput, calls=%fused_computation.45 | convolution fusion | flops 135397376 | bytes 2891776 | tf_op jit(solution)/shard_map/while/body/eval_jaxpr/grqk,qgrd->kgd/dot_general | solution.py:57
  76.7 1.1 fusion.39
  77.9 1.1 slice-done.1
  79.0 1.8 %fusion.2 = f32[256,3072]{1,0:T(8,128)S(1)} fusion(bf16[256,1024]{0,1:T(8,128)(2,1)S(1)} %bitcast.152, bf16[1,3072,1024]{2,1,0:T(8,128)(2,1)S(1)} %bitcast.140), kind=kOutput, calls=%fused_computation.2 | convolution fusion | flops 1610612736 | bytes 9961472 | tf_op jit(solution)/shard_map/dot_general | solution.py:161
  81.0 1.1 convolution_add_fusion.1
  82.1 2.2 %fusion.6 = bf16[256,3072]{1,0:T(8,128)(2,1)} fusion(f32[256,3072]{1,0:T(8,128)S(1)} %convolution_add_fusion.1, bf16[256,512]{0,1:T(8,128)(2,1)S(1)} %bitcast.147, bf16[1,3072,512]{2,1,0:T(8,128)(2,1)S(1)} %copy-done), kind=kOutput, calls=%fused_computation.11 | convolution fusion | flops 806879232 | bytes 8126464 | tf_op jit(solution)/shard_map/dot_general | solution.py:168
  84.3 27.0 %all-reduce.2.cloned.1.call-done = f32[64,3072]{1,0:T(8,128)} async-done(((f32[64,3072]{1,0:T(8,128)}), f32[64,3072]{1,0:T(8,128)}) %all-reduce.2.cloned.1.call-update) | async-done | bytes 786448 | tf_op jit(solution)/shard_map/psum | solution.py:185
  111.3 3.1 %multiply_subtract_fusion = (f32[64,3072]{1,0:T(8,128)}, f32[64,3072]{1,0:T(8,128)}) fusion(f32[64,3072]{1,0:T(8,128)} %param.15, f32[64,3072]{1,0:T(8,128)} %all-reduce.2.cloned.1.call-done, f32[64,3072]{1,0:T(8,128)} %param.16), kind=kLoop, calls=%fused_computation.66 | loop fusion | flops 1376256 | bytes 3932160 | tf_op jit(solution)/shard_map/sub | solution.py:187
  114.7 1.2 copy-done.2
  115.9 2.9 %fusion.5 = bf16[1,3072,512]{2,1,0:T(8,128)(2,1)} fusion(bf16[256,3072]{1,0:T(8,128)(2,1)S(1)} %copy-done.2, bf16[256,512]{0,1:T(8,128)(2,1)S(1)} %bitcast.148), kind=kOutput, calls=%fused_computation.8 | convolution fusion | flops 806879232 | bytes 4980736 | tf_op jit(solution)/shard_map/dot_general | solution.py:157
  118.8 2.7 %fusion.4 = bf16[1,3072,512]{2,1,0:T(8,128)(2,1)} fusion(bf16[256,3072]{1,0:T(8,128)(2,1)S(1)} %copy-done.2, bf16[256,512]{0,1:T(8,128)(2,1)S(1)} %bitcast.144), kind=kOutput, calls=%fused_computation.7 | convolution fusion | flops 806879232 | bytes 4980736 | tf_op jit(solution)/shard_map/dot_general | solution.py:154
  121.5 4.6 %convert_bitcast_fusion = bf16[1,3072,1024]{2,1,0:T(8,128)(2,1)} fusion(bf16[256,3072]{1,0:T(8,128)(2,1)S(1)} %copy-done.2, bf16[256,1024]{0,1:T(8,128)(2,1)S(1)} %fusion.37), kind=kOutput, calls=%fused_computation.4 | convolution fusion | flops 1613758464 | bytes 8388608 | tf_op jit(solution)/shard_map/dot_general | solution.py:151
  126.1 1.9 %fusion.24 = (f32[128]{0:T(128)S(1)}, f32[3072]{0:T(1024)S(1)}) fusion(bf16[128,3072]{1,0:T(8,128)(2,1)} %reduce-scatter.2.cloned.1.call-done, bf16[1,128,3072]{2,1,0:T(8,128)(2,1)} %param.9, f32[3072]{0:T(1024)S(1)} %bitcast.154, f32[128]{0:T(128)S(1)} %add_rsqrt_fusion), kind=kLoop, calls=%fused_computation.36 | loop fusion | flops 3142528 | bytes 1598464 | tf_op jit(solution)/shard_map/reduce_sum | solution.py:180
  128.0 8.8 %psum.14 = f32[1,3072]{1,0:T(1,128)} all-reduce(f32[1,3072]{1,0:T(1,128)S(1)} %bitcast.156), channel_id=1, replica_groups=mesh['rep'=16,'tp'=2] {'tp'}, use_global_device_ids=true, to_apply=%region_6.7 | all-reduce | flops 3072 | bytes 24576 | tf_op jit(solution)/shard_map/psum | solution.py:174
  136.8 2.7 %fusion.46 = bf16[1,128,3072]{2,1,0:T(8,128)(2,1)} fusion(bf16[128,3072]{1,0:T(8,128)(2,1)} %reduce-scatter.2.cloned.1.call-done, bf16[1,128,3072]{2,1,0:T(8,128)(2,1)} %param.9, f32[128]{0:T(128)S(1)} %broadcast_multiply_fusion.1, f32[3072]{0:T(1024)S(1)} %bitcast.155, f32[128]{0:T(128)S(1)} %add_rsqrt_fusion), kind=kLoop, calls=%fused_computation.64 | loop fusion | flops 3145728 | bytes 2372608 | tf_op jit(solution)/shard_map/broadcast_in_dim | solution.py:193
  (65 shorter events, 4.3 us)
Async XLA Ops:
  8.0 43.5 %copy-start = (bf16[1,3072,512]{2,1,0:T(8,128)(2,1)S(1)}, bf16[1,3072,512]{2,1,0:T(8,128)(2,1)}, u32[]{:S(2)}) copy-start(bf16[1,3072,512]{2,1,0:T(8,128)(2,1)} %param.13) | copy-start | bytes 9437188
  8.0 4.0 %copy-start.19 = (bf16[1,64,3072]{2,1,0:T(8,128)(2,1)S(1)}, bf16[1,64,3072]{2,1,0:T(8,128)(2,1)}, u32[]{:S(2)}) copy-start(bf16[1,64,3072]{2,1,0:T(8,128)(2,1)} %param.17) | copy-start | bytes 1179652
  8.0 34.0 %all-gather.2.cloned.1.call-start = ((), (), s32[]{:S(2)}) async-start(), calls=%async_computation.1 | async-start | bytes 2359296 | tf_op jit(solution)/shard_map/all_gather | solution.py:106
  11.9 99.4 %all-reduce.2.cloned.1.call-start = ((), (), s32[]{:S(2)}) async-start(), calls=%async_computation.3 | async-start | bytes 1572864 | tf_op jit(solution)/shard_map/psum | solution.py:185
  14.1 112.0 %reduce-scatter.2.cloned.1.call-start = ((), (), s32[]{:S(2)}) async-start(), calls=%async_computation.2 | async-start | bytes 2359296 | tf_op jit(solution)/shard_map/reduce_scatter | solution.py:165
  42.0 6.4 %copy-start.8 = (bf16[512,3072]{1,0:T(8,128)(2,1)S(1)}, bf16[512,3072]{1,0:T(8,128)(2,1)}, u32[]{:S(2)}) copy-start(bf16[512,3072]{1,0:T(8,128)(2,1)} %copy.35) | copy-start | bytes 9437188
  47.3 3.2 %copy-start.7 = (f32[256,8,128]{0,2,1:T(8,128)}, f32[256,8,128]{0,2,1:T(8,128)S(1)}, u32[]{:S(2)}) copy-start(f32[256,8,128]{0,2,1:T(8,128)S(1)} %fusion.26) | copy-start | bytes 3145732
  47.3 2.2 %copy-start.1 = (bf16[256,3072]{1,0:T(8,128)(2,1)S(1)}, bf16[256,3072]{1,0:T(8,128)(2,1)}, u32[]{:S(2)}) copy-start(bf16[256,3072]{1,0:T(8,128)(2,1)} %all-gather.2.cloned.1.call-done) | copy-start | bytes 4718596
  50.5 1.0 copy-start.9
  55.0 2.7 %copy-start.10 = (f32[256,4,128]{0,2,1:T(8,128)S(1)}, f32[256,4,128]{0,2,1:T(8,128)}, u32[]{:S(2)}) copy-start(f32[256,4,128]{0,2,1:T(8,128)} %copy-done.9) | copy-start | bytes 1572868
  55.0 2.7 %copy-start.14 = (f32[256,4,64]{0,2,1:T(8,128)S(1)}, f32[256,4,64]{0,2,1:T(8,128)}, u32[]{:S(2)}) copy-start(f32[256,4,64]{0,2,1:T(8,128)} %get-tuple-element.43) | copy-start | bytes 786436
  55.0 2.7 %copy-start.15 = (f32[256,4,64]{0,2,1:T(8,128)S(1)}, f32[256,4,64]{0,2,1:T(8,128)}, u32[]{:S(2)}) copy-start(f32[256,4,64]{0,2,1:T(8,128)} %get-tuple-element.44) | copy-start | bytes 786436
  55.0 3.5 %copy-start.11 = (bf16[1,256,1024]{1,2,0:T(8,128)(2,1)S(1)}, bf16[1,256,1024]{1,2,0:T(8,128)(2,1)}, u32[]{:S(2)}) copy-start(bf16[1,256,1024]{1,2,0:T(8,128)(2,1)} %copy.41) | copy-start | bytes 1572868
  55.0 3.5 %copy-start.16 = (bf16[256,4,128]{2,1,0:T(4,128)(2,1)S(1)}, bf16[256,4,128]{2,1,0:T(4,128)(2,1)}, u32[]{:S(2)}) copy-start(bf16[256,4,128]{2,1,0:T(4,128)(2,1)} %reshape.115) | copy-start | bytes 786436
  74.2 2.3 %copy-start.17 = (f32[256,4,128]{0,2,1:T(8,128)S(1)}, f32[256,4,128]{0,2,1:T(8,128)}, u32[]{:S(2)}) copy-start(f32[256,4,128]{0,2,1:T(8,128)} %get-tuple-element.49) | copy-start | bytes 1572868
  74.2 2.4 %copy-start.4 = (f32[4,128,2,256]{3,1,2,0:T(8,128)S(1)}, f32[4,128,2,256]{3,1,2,0:T(8,128)}, u32[]{:S(2)}) copy-start(f32[4,128,2,256]{3,1,2,0:T(8,128)} %fusion.44) | copy-start | bytes 3145732
  74.2 3.7 %slice-start = ((s8[6291456]{0:T(1024)(128)(4,1)}), s8[4194304]{0:T(1024)(128)(4,1)S(1)}, s32[]{:S(2)}) async-start(s8[6291456]{0:T(1024)(128)(4,1)} %bitcast.139), calls=%async_computation.4 | async-start | bytes 8388608
  76.5 5.6 %copy-start.12 = (bf16[4,256,128]{1,2,0:T(8,128)(2,1)}, bf16[4,256,128]{1,2,0:T(8,128)(2,1)S(1)}, u32[]{:S(2)}) copy-start(bf16[4,256,128]{1,2,0:T(8,128)(2,1)S(1)} %fusion.33) | copy-start | bytes 786436
  76.5 2.5 %slice-start.1 = ((s8[6291456]{0:T(1024)(128)(4,1)}), s8[2097152]{0:T(1024)(128)(4,1)S(1)}, s32[]{:S(2)}) async-start(s8[6291456]{0:T(1024)(128)(4,1)} %bitcast.139), calls=%async_computation.5 | async-start | bytes 4194304
  79.0 1.9 %copy-start.18 = (f32[256,4,128]{0,2,1:T(8,128)S(1)}, f32[256,4,128]{0,2,1:T(8,128)}, u32[]{:S(2)}) copy-start(f32[256,4,128]{0,2,1:T(8,128)} %get-tuple-element.50) | copy-start | bytes 1572868
  79.0 2.1 %copy-start.3 = (bf16[1,3072,512]{2,1,0:T(8,128)(2,1)S(1)}, bf16[1,3072,512]{2,1,0:T(8,128)(2,1)}, u32[]{:S(2)}) copy-start(bf16[1,3072,512]{2,1,0:T(8,128)(2,1)} %param.12) | copy-start | bytes 9437188
  111.3 3.1 %copy-start.5 = (f32[4,128,2,256]{3,1,2,0:T(8,128)S(1)}, f32[4,128,2,256]{3,1,2,0:T(8,128)}, u32[]{:S(2)}) copy-start(f32[4,128,2,256]{3,1,2,0:T(8,128)} %fusion.44) | copy-start | bytes 3145732
  111.3 3.1 %copy-start.6 = (f32[256,8,128]{0,2,1:T(8,128)S(1)}, f32[256,8,128]{0,2,1:T(8,128)}, u32[]{:S(2)}) copy-start(f32[256,8,128]{0,2,1:T(8,128)} %get-tuple-element.36) | copy-start | bytes 3145732
  114.5 1.4 copy-start.2
  114.5 1.4 copy-start.13
  121.5 4.6 %copy-start.20 = (f32[1,3072]{1,0:T(1,128)S(1)}, f32[1,3072]{1,0:T(1,128)}, u32[]{:S(2)}) copy-start(f32[1,3072]{1,0:T(1,128)} %param.10) | copy-start | bytes 36868
Sparse Core Ops, SparseCore 0:
  12.1 29.9 all-gather.1
  84.5 26.1 reduce-scatter.1
Sparse Core Ops, SparseCore 1:
  16.4 94.9 all-reduce.1
where the time goes:
time: 148 us; the launch traced here: 147 us
  matrix products  41.3 us (28%)
  waiting for transfers between devices  38.9 us (26%)
  other arithmetic  21.3 us (14%)
  local copies, waits for them, and re-layouts  20.8 us (14%)
  between operations  15.7 us (11%)
  blocking collectives  8.76 us (6%)
    psum x1, waiting for transfers between devices, body(): mean_delta = lax.psum(delta, 'rep') / replicas  27 us
    all_gather x1, waiting for transfers between devices, body(): normalized = lax.all_gather(normalized_local, 'tp', axis=0, tiled=True)  11.8 us
    psum x1, blocking collectives, body(): lax.psum(jnp.sum(summed_rows * normalized_input, axis=0), 'tp')  8.76 us
    dot_general x1, local copies, waits for them, and re-layouts, body(): jnp.dot(normalized, weight_q, preferred_element_type=jnp.float32)  8.68 us
    dot_general x1, matrix products, one_block(): jnp.einsum('grqk,qgrd->kgd', score_low, query_block, preferred_element_ty...  5.36 us
    dot_general x1, matrix products, one_block(): jnp.einsum('grqk,kgd->qgrd', score_low, rotated_keys, preferred_element_t...  5.3 us
    dot_general x1, matrix products, body(): jnp.dot(normalized, weight_q, preferred_element_type=jnp.float32)  5.26 us
    dot_general x1, local copies, waits for them, and re-layouts, body(): jnp.dot(normalized, weight_k, preferred_element_type=jnp.float32)  4.69 us
  transfers between devices with their start and end apart: 3, of which 2 were waited for; matrix products, arithmetic and copies ran while one was open for 49% of the time, Pallas kernels for 0%

commit v1 on v0

--- a/solution.py
+++ b/solution.py
@@ -8,6 +8,12 @@
 rope_base = 500000.0
 outer_rate = 0.7
 outer_momentum = 0.9
+
+
+def gather_and_add(shard, axis):
+    parts = lax.all_gather(shard, axis, axis=0, tiled=False)
+    acc = parts.sum(axis=0)
+    return acc
 
 
 def rope_tables(sequence_length, width):
@@ -182,7 +188,7 @@
     ).astype(jnp.bfloat16)
     delta = global_fragment - local_fragment[0].astype(jnp.float32)
     replicas = lax.axis_size("rep")
-    mean_delta = lax.psum(delta, "rep") / replicas
+    mean_delta = gather_and_add(delta, "rep") / replicas
     new_momentum = outer_momentum * momentum + mean_delta
     new_global = global_fragment - outer_rate * (mean_delta + outer_momentum * new_momentum)
     return (

time: 148 us -> 210 us (1.42)
  waiting for transfers between devices: 38.9 us -> 91.1 us
  other arithmetic: 21.3 us -> 28 us
  matrix products: 41.3 us -> 47.8 us
  local copies, waits for them, and re-layouts: 20.8 us -> 18.4 us
    all_gather x0 -> x1, waiting for transfers between devices: none -> 65.1 us  [gather_and_add(): parts = lax.all_gather(shard, axis, axis=0, tiled=False)]
    psum x1 -> x0, waiting for transfers between devices: 27 us -> none  [body(): mean_delta = lax.psum(delta, 'rep') / replicas]
    reduce_scatter x1, waiting for transfers between devices: 0.01 us -> 11.8 us  [body(): lax.psum_scatter((partial_value + lax.dot_general(value_gradient, weight_...]
    reduce_sum x0 -> x1, other arithmetic: none -> 6.27 us  [gather_and_add(): acc = parts.sum(axis=0)]
    dot_general x1, matrix products: 1.84 us -> 4.85 us  [body(): lax.dot_general(dquery, weight_q, back, preferred_element_type=jnp.float32)]
    dot_general x1, matrix products: 1.05 us -> 3.49 us  [body(): jnp.dot(normalized, weight_k, preferred_element_type=jnp.float32)]
    unnamed x46 -> x22, local copies, waits for them, and re-layouts: 3.6 us -> 1.3 us
    all_gather x1, waiting for transfers between devices: 11.8 us -> 14.1 us  [body(): normalized = lax.all_gather(normalized_local, 'tp', axis=0, tiled=True)]
  transfers between devices with their start and end apart: 3 -> 3, of which waited for: 2 -> 3; matrix products, arithmetic and copies ran while one was open for 49% -> 17% of each run, Pallas kernels for 0% -> 0%
where the time goes in v1:
time: 210 us; the launch traced here: 209 us
  waiting for transfers between devices  91.1 us (43%)
  matrix products  47.8 us (23%)
  other arithmetic  28 us (13%)
  local copies, waits for them, and re-layouts  18.4 us (9%)
  between operations  15.7 us (7%)
  blocking collectives  7.54 us (4%)
    all_gather x1, waiting for transfers between devices, gather_and_add(): parts = lax.all_gather(shard, axis, axis=0, tiled=False)  65.1 us
    all_gather x1, waiting for transfers between devices, body(): normalized = lax.all_gather(normalized_local, 'tp', axis=0, tiled=True)  14.1 us
    reduce_scatter x1, waiting for transfers between devices, body(): lax.psum_scatter((partial_value + lax.dot_general(value_gradient, weight_...  11.8 us
    dot_general x1, local copies, waits for them, and re-layouts, body(): jnp.dot(normalized, weight_q, preferred_element_type=jnp.float32)  8.68 us
    psum x1, blocking collectives, body(): lax.psum(jnp.sum(summed_rows * normalized_input, axis=0), 'tp')  7.54 us
    reduce_sum x1, other arithmetic, gather_and_add(): acc = parts.sum(axis=0)  6.27 us
    dot_general x1, matrix products, one_block(): jnp.einsum('grqk,qgrd->kgd', score_low, query_block, preferred_element_ty...  5.35 us
    dot_general x1, matrix products, one_block(): jnp.einsum('grqk,kgd->qgrd', score_low, rotated_keys, preferred_element_t...  5.26 us
  transfers between devices with their start and end apart: 3, of which 3 were waited for; matrix products, arithmetic and copies ran while one was open for 17% of the time, Pallas kernels for 0%

profile of v1, /device:TPU:0, one launch (start us, length us, event | category | flops | bytes accessed | tf_op | source)
XLA Modules:
  0.0 208.7 jit_solution(5767906690166812729)
XLA Ops:
  8.1 1.5 fusion.25
  9.6 2.3 %fusion.22 = bf16[128,3072]{1,0:T(8,128)(2,1)} fusion(bf16[1,128,3072]{2,1,0:T(8,128)(2,1)} %param.9, f32[3072]{0:T(1024)} %bitcast.153, f32[128]{0:T(128)S(1)} %add_rsqrt_fusion), kind=kLoop, calls=%fused_computation.34 | loop fusion | flops 1572864 | bytes 1585664 | tf_op jit(solution)/shard_map/convert_element_type | solution.py:111
  12.0 2.0 copy.41
  14.0 4.6 %copy.35 = bf16[512,3072]{1,0:T(8,128)(2,1)} copy(bf16[512,3072]{0,1:T(8,128)(2,1)} %bitcast.139) | data formatting | bytes 6291456 | tf_op jit(solution)/shard_map/dot_general | solution.py:121
  18.6 8.7 %copy.38 = bf16[1024,3072]{1,0:T(8,128)(2,1)} copy(bf16[1024,3072]{0,1:T(8,128)(2,1)} %bitcast.140) | data formatting | bytes 12582912 | tf_op jit(solution)/shard_map/dot_general | solution.py:117
  27.9 14.1 %all-gather.4.cloned.1.call-done = bf16[256,3072]{1,0:T(8,128)(2,1)} async-done(((bf16[128,3072]{1,0:T(8,128)(2,1)}), bf16[256,3072]{1,0:T(8,128)(2,1)}) %all-gather.4.cloned.1.call-update) | async-done | bytes 1572880 | tf_op jit(solution)/shard_map/all_gather | solution.py:112
  42.0 3.1 %fusion.30 = bf16[256,512]{1,0:T(8,128)(2,1)} fusion(bf16[256,3072]{1,0:T(8,128)(2,1)} %all-gather.4.cloned.1.call-done, bf16[1,3072,512]{2,1,0:T(8,128)(2,1)S(1)} %copy-done), kind=kOutput, calls=%fused_computation.44 | convolution fusion | flops 805437440 | bytes 4980736 | tf_op jit(solution)/shard_map/dot_general | solution.py:126
  45.1 1.7 reshape.115
  46.8 3.5 %fusion.28 = f32[256,4,128]{0,2,1:T(8,128)S(1)} fusion(bf16[4,128,3072]{2,1,0:T(8,128)(2,1)} %bitcast.142, bf16[256,3072]{1,0:T(8,128)(2,1)} %all-gather.4.cloned.1.call-done), kind=kOutput, calls=%fused_computation.40 | convolution fusion | flops 805306368 | bytes 5242880 | tf_op jit(solution)/shard_map/dot_general | solution.py:121
  50.3 4.6 %fusion.26 = f32[256,8,128]{0,2,1:T(8,128)S(1)} fusion(bf16[8,128,3072]{2,1,0:T(8,128)(2,1)} %bitcast.141, bf16[256,3072]{1,0:T(8,128)(2,1)S(1)} %copy-done.1), kind=kOutput, calls=%fused_computation.38 | convolution fusion | flops 1610612736 | bytes 8912896 | tf_op jit(solution)/shard_map/dot_general | solution.py:117
  56.1 1.7 fusion.51
  59.6 3.3 %fusion.65 = (f32[4,2,256]{2,1,0:T(2,128)S(1)}, f32[4,2,256,256]{2,3,1,0:T(8,128)}) fusion(pred[256,256]{0,1:T(8,128)(4,1)S(1)} %iota_compare_fusion, bf16[256,4,128,1]{0,2,3,1:T(8,128)(2,1)} %fusion.50, bf16[256,4,2,128]{0,3,2,1:T(8,128)(2,1)} %bitcast.150), kind=kOutput, calls=%fused_computation.98 | convolution fusion | flops 136315136 | bytes 2957312 | tf_op jit(solution)/shard_map/while/body/eval_jaxpr/sub | solution.py:60
  62.9 2.9 %fusion.33 = bf16[4,256,128]{1,2,0:T(8,128)(2,1)} fusion(bf16[256,4,2,128]{0,3,2,1:T(8,128)(2,1)} %bitcast.145, f32[4,2,256,256]{2,3,1,0:T(8,128)} %get-tuple-element.48, f32[4,2,256]{2,1,0:T(2,128)S(1)} %get-tuple-element.47), kind=kOutput, calls=%fused_computation.45 | convolution fusion | flops 135397376 | bytes 2891776 | tf_op jit(solution)/shard_map/while/body/eval_jaxpr/grqk,qgrd->kgd/dot_general | solution.py:63
  65.8 5.4 %broadcast_multiply_fusion = (f32[256,4,128]{0,2,1:T(8,128)}, f32[256,4,128]{0,2,1:T(8,128)}) fusion(f32[256,128]{0,1:T(8,128)S(1)} %get-tuple-element.46, bf16[256,4,2,128]{0,3,2,1:T(8,128)(2,1)} %bitcast.151, f32[4,256,256,2]{2,1,3,0:T(8,128)} %fusion.51, f32[4,2,256,256]{2,3,1,0:T(8,128)} %get-tuple-element.48, f32[4,2,256]{2,1,0:T(2,128)S(1)} %get-tuple-element.47), kind=kOutput, calls=%fused_computation.81 | convolution fusion | flops 138021120 | bytes 5906432 | tf_op jit(solution)/shard_map/while/body/eval_jaxpr/grqk,qgrd->kgd/dot_general | solution.py:78
  71.1 5.3 %fusion.44 = f32[4,128,2,256]{3,1,2,0:T(8,128)} fusion(bf16[256,4,128,1]{0,2,3,1:T(8,128)(2,1)} %fusion.50, f32[4,256,256,2]{2,1,3,0:T(8,128)} %fusion.51, f32[4,2,256,256]{2,3,1,0:T(8,128)} %get-tuple-element.48, f32[4,2,256]{2,1,0:T(2,128)S(1)} %get-tuple-element.47), kind=kOutput, calls=%fused_computation.62 | convolution fusion | flops 137890048 | bytes 5513216 | tf_op jit(solution)/shard_map/while/body/eval_jaxpr/grqk,kgd->qgrd/dot_general | solution.py:75
  76.4 1.1 fusion.64
  77.5 1.4 bitcast_multiply_fusion.3
  79.0 1.1 fusion.39
  80.2 4.8 %fusion.2 = f32[256,3072]{1,0:T(8,128)S(1)} fusion(bf16[256,1024]{0,1:T(8,128)(2,1)S(1)} %bitcast.152, bf16[1,3072,1024]{2,1,0:T(8,128)(2,1)} %param.11), kind=kOutput, calls=%fused_computation.2 | convolution fusion | flops 1610612736 | bytes 9961472 | tf_op jit(solution)/shard_map/dot_general | solution.py:167
  86.2 2.2 %fusion.6 = bf16[256,3072]{1,0:T(8,128)(2,1)} fusion(f32[256,3072]{1,0:T(8,128)S(1)} %convolution_add_fusion.1, bf16[256,512]{0,1:T(8,128)(2,1)S(1)} %bitcast.147, bf16[1,3072,512]{2,1,0:T(8,128)(2,1)S(1)} %copy-done), kind=kOutput, calls=%fused_computation.11 | convolution fusion | flops 806879232 | bytes 8126464 | tf_op jit(solution)/shard_map/dot_general | solution.py:174
  88.7 2.2 %convert_subtract_fusion = f32[64,3072]{1,0:T(8,128)} fusion(f32[64,3072]{1,0:T(8,128)} %param.15, bf16[1,64,3072]{2,1,0:T(8,128)(2,1)} %param.17), kind=kLoop, calls=%fused_computation.65 | loop fusion | flops 393216 | bytes 1966080 | tf_op jit(solution)/shard_map/sub | solution.py:189
  90.9 1.8 fusion.37
  92.9 2.7 %fusion.5 = bf16[1,3072,512]{2,1,0:T(8,128)(2,1)} fusion(bf16[256,3072]{1,0:T(8,128)(2,1)S(1)} %copy-done.2, bf16[256,512]{0,1:T(8,128)(2,1)S(1)} %bitcast.148), kind=kOutput, calls=%fused_computation.8 | convolution fusion | flops 806879232 | bytes 4980736 | tf_op jit(solution)/shard_map/dot_general | solution.py:163
  95.6 2.7 %fusion.4 = bf16[1,3072,512]{2,1,0:T(8,128)(2,1)} fusion(bf16[256,3072]{1,0:T(8,128)(2,1)S(1)} %copy-done.2, bf16[256,512]{0,1:T(8,128)(2,1)S(1)} %bitcast.144), kind=kOutput, calls=%fused_computation.7 | convolution fusion | flops 806879232 | bytes 4980736 | tf_op jit(solution)/shard_map/dot_general | solution.py:160
  98.3 4.6 %convert_bitcast_fusion = bf16[1,3072,1024]{2,1,0:T(8,128)(2,1)} fusion(bf16[256,3072]{1,0:T(8,128)(2,1)S(1)} %copy-done.2, bf16[256,1024]{0,1:T(8,128)(2,1)S(1)} %fusion.37), kind=kOutput, calls=%fused_computation.4 | convolution fusion | flops 1613758464 | bytes 8388608 | tf_op jit(solution)/shard_map/dot_general | solution.py:157
  102.9 11.8 %reduce-scatter.2.cloned.1.call-done = bf16[128,3072]{1,0:T(8,128)(2,1)} async-done(((bf16[256,3072]{1,0:T(8,128)(2,1)}), bf16[128,3072]{1,0:T(8,128)(2,1)}) %reduce-scatter.2.cloned.1.call-update) | async-done | bytes 786448 | tf_op jit(solution)/shard_map/reduce_scatter | solution.py:171
  114.7 1.9 fusion.24
  116.7 7.5 %psum.7 = f32[1,3072]{1,0:T(1,128)} all-reduce(f32[1,3072]{1,0:T(1,128)S(1)} %bitcast.156), channel_id=1, replica_groups=mesh['rep'=16,'tp'=2] {'tp'}, use_global_device_ids=true, to_apply=%region_6.7 | all-reduce | flops 3072 | bytes 24576 | tf_op jit(solution)/shard_map/psum | solution.py:180
  124.2 2.7 %fusion.46 = bf16[1,128,3072]{2,1,0:T(8,128)(2,1)} fusion(bf16[128,3072]{1,0:T(8,128)(2,1)} %reduce-scatter.2.cloned.1.call-done, bf16[1,128,3072]{2,1,0:T(8,128)(2,1)} %param.9, f32[128]{0:T(128)S(1)} %broadcast_multiply_fusion.1, f32[3072]{0:T(1024)S(1)} %bitcast.155, f32[128]{0:T(128)S(1)} %add_rsqrt_fusion), kind=kLoop, calls=%fused_computation.64 | loop fusion | flops 3145728 | bytes 2372608 | tf_op jit(solution)/shard_map/broadcast_in_dim | solution.py:199
  126.9 65.1 %all-gather.6.cloned.1.call-done = f32[1024,3072]{1,0:T(8,128)} async-done(((f32[64,3072]{1,0:T(8,128)}), f32[1024,3072]{1,0:T(8,128)}) %all-gather.6.cloned.1.call-update) | async-done | bytes 12582928 | tf_op jit(solution)/shard_map/all_gather | solution.py:14
  192.1 6.3 %reduce_sum.61 = f32[64,3072]{1,0:T(8,128)} reduce(f32[16,64,3072]{2,1,0:T(8,128)} %bitcast.138, f32[]{:T(128)} %constant.15.clone.1), dimensions={0}, to_apply=%region_8.9 | reduce | flops 2949120 | bytes 13369348 | tf_op jit(solution)/shard_map/reduce_sum | solution.py:15
  198.3 3.0 %multiply_subtract_fusion = (f32[64,3072]{1,0:T(8,128)}, f32[64,3072]{1,0:T(8,128)}) fusion(f32[64,3072]{1,0:T(8,128)} %param.15, f32[64,3072]{1,0:T(8,128)} %reduce_sum.61, f32[64,3072]{1,0:T(8,128)} %param.16), kind=kLoop, calls=%fused_computation.66 | loop fusion | flops 1376256 | bytes 3932160 | tf_op jit(solution)/shard_map/sub | solution.py:193
  (41 shorter events, 5.4 us)
Async XLA Ops:
  8.0 34.0 %copy-start = (bf16[1,3072,512]{2,1,0:T(8,128)(2,1)S(1)}, bf16[1,3072,512]{2,1,0:T(8,128)(2,1)}, u32[]{:S(2)}) copy-start(bf16[1,3072,512]{2,1,0:T(8,128)(2,1)} %param.13) | copy-start | bytes 9437188
  8.0 34.0 %all-gather.4.cloned.1.call-start = ((), (), s32[]{:S(2)}) async-start(), calls=%async_computation.1 | async-start | bytes 2359296 | tf_op jit(solution)/shard_map/all_gather | solution.py:112
  11.9 102.8 %reduce-scatter.2.cloned.1.call-start = ((), (), s32[]{:S(2)}) async-start(), calls=%async_computation.2 | async-start | bytes 2359296 | tf_op jit(solution)/shard_map/reduce_scatter | solution.py:171
  46.8 3.6 %copy-start.1 = (bf16[256,3072]{1,0:T(8,128)(2,1)S(1)}, bf16[256,3072]{1,0:T(8,128)(2,1)}, u32[]{:S(2)}) copy-start(bf16[256,3072]{1,0:T(8,128)(2,1)} %all-gather.4.cloned.1.call-done) | copy-start | bytes 4718596
  55.0 1.0 copy-start.5
  55.0 1.1 copy-start.8
  77.5 1.5 copy-start.4
  80.1 4.9 %copy-start.9 = (f32[256,4,128]{0,2,1:T(8,128)S(1)}, f32[256,4,128]{0,2,1:T(8,128)}, u32[]{:S(2)}) copy-start(f32[256,4,128]{0,2,1:T(8,128)} %get-tuple-element.50) | copy-start | bytes 1572868
  80.2 5.0 %copy-start.3 = (bf16[1,3072,512]{2,1,0:T(8,128)(2,1)S(1)}, bf16[1,3072,512]{2,1,0:T(8,128)(2,1)}, u32[]{:S(2)}) copy-start(bf16[1,3072,512]{2,1,0:T(8,128)(2,1)} %param.12) | copy-start | bytes 9437188
  85.1 1.1 copy-start.6
  88.4 103.6 %all-gather.6.cloned.1.call-start = ((), (), s32[]{:S(2)}) async-start(), calls=%async_computation.3 | async-start | bytes 13369344 | tf_op jit(solution)/shard_map/all_gather | solution.py:14
  90.9 2.0 copy-start.2
  90.9 2.0 copy-start.7
  98.3 16.4 %copy-start.10 = (f32[1,3072]{1,0:T(1,128)S(1)}, f32[1,3072]{1,0:T(1,128)}, u32[]{:S(2)}) copy-start(f32[1,3072]{1,0:T(1,128)} %param.10) | copy-start | bytes 36868
Sparse Core Ops, SparseCore 0:
  12.0 29.8 all-gather.3
  88.6 26.1 reduce-scatter.1
Sparse Core Ops, SparseCore 1:
  91.8 100.2 all-gather.5
